TPU v7x, 32 devices: a whole 2x2x4 slice. The times are simulated.
32 devices in a mesh: terms: 2 (over x), rows: 4 (over y, core), cols: 4 (over z).
Axes of the slice: x: 2, y: 2, z: 4, core: 2. Of those that a mesh axis runs over, the one named last changes fastest.
Arguments:
- wavefunction: bfloat16 [2, 1024, 1024], P(None, 'rows', 'cols'), may hold values from -6 to 6
- energy: float32 [2], replicated, may hold values from 1 to 4
- block_rows: int32 [2], replicated, may hold values from 512 to 1024
- block_cols: int32 [2], replicated, may hold values from 512 to 1024
- left_ops: bfloat16 [8, 1024, 1024], P('terms', 'rows'), may hold values from -0.1875 to 0.1875
- right_ops: bfloat16 [8, 1024, 1024], P('terms', 'cols'), may hold values from -0.1875 to 0.1875
- source: int32 [8], P('terms'), may hold values from 0 to 1
- target: int32 [8], P('terms'), may hold values from 0 to 1
Outputs:
- sigma: bfloat16 [2, 1024, 1024], P(None, 'rows', 'cols')
- residual: bfloat16 [2, 1024, 1024], P(None, 'rows', 'cols')
Inputs may be any that keep to these rules, and one draw needn't show every extreme that they name: source[t] is the sector whose block term t reads. target[t] is the sector to which term t adds. `block_rows`: entries of a sector block beyond its live left or right states are ignored.
All inputs are finite; a program needn't handle non-finite values.
Results may differ from a plain program's by a relative error of at most 0.0044.
The roundings to bfloat16 on the way count: a program that leaves them out, or rounds other values in their place, can miss the bound.
Values may be sent and summed in bfloat16 or wider, within the bound.
No kernel may reach another device: no remote copies, remote signals or barrier semaphores. Data moves between devices by JAX's collectives and lax.ppermute only.
A program may use at most 64 MiB of HBM per device.

v0:
```python
import jax
import jax.numpy as jnp
from jax import lax
from jax.sharding import PartitionSpec as P

EPSILON = 1e-06


def per_device(wavefunction, energy, block_rows, block_cols, left_ops, right_ops, source, target):
    sectors, tile_rows, tile_cols = wavefunction.shape
    term_count = left_ops.shape[0]
    row_ids = lax.axis_index("rows") * tile_rows + lax.iota(jnp.int32, tile_rows)
    col_ids = lax.axis_index("cols") * tile_cols + lax.iota(jnp.int32, tile_cols)
    inside = (row_ids[None, :, None] < block_rows[:, None, None]) & (
        col_ids[None, None, :] < block_cols[:, None, None]
    )
    live_psi = jnp.where(inside, wavefunction, jnp.zeros_like(wavefunction))
    sector_ids = lax.iota(jnp.int32, sectors)
    partial_value = jnp.zeros((sectors, tile_rows, tile_cols), jnp.float32)
    panels = lax.all_gather(live_psi, "rows", axis=1, tiled=True)
    product_list = []
    for term_index in range(term_count):
        col_panel = lax.dynamic_index_in_dim(panels, source[term_index], 0, keepdims=False)
        product_list.append(
            jnp.dot(left_ops[term_index], col_panel, preferred_element_type=jnp.float32).astype(
                jnp.bfloat16
            )
        )
    products = jnp.stack(product_list)
    additions = jnp.einsum(
        "txl,tml->txm",
        lax.all_gather(products, "cols", axis=2, tiled=True),
        right_ops,
        preferred_element_type=jnp.float32,
    )
    for term_index in range(term_count):
        hit = (sector_ids == target[term_index])[:, None, None]
        partial_value = partial_value + jnp.where(hit, additions[term_index][None], 0.0)
    live_f = live_psi.astype(jnp.float32)
    summed = lax.psum(partial_value, "terms")
    full_sigma = jnp.where(inside, summed + energy[:, None, None] * live_f, 0.0)
    numerator, denominator = lax.psum(
        (jnp.sum(live_f * full_sigma), jnp.sum(live_f * live_f)), ("rows", "cols")
    )
    rayleigh = numerator / (denominator + EPSILON)
    residual = full_sigma - rayleigh * live_f
    return (full_sigma.astype(jnp.bfloat16), residual.astype(jnp.bfloat16))


def solution(mesh):
    in_specs = (
        P(None, "rows", "cols"),
        P(),
        P(),
        P(),
        P("terms", "rows", None),
        P("terms", "cols", None),
        P("terms"),
        P("terms"),
    )
    out_specs = (P(None, "rows", "cols"), P(None, "rows", "cols"))
    return jax.shard_map(
        per_device, mesh=mesh, in_specs=in_specs, out_specs=out_specs, check_vma=False
    )
```

profile of v0, /device:TPU:0, one launch (start us, length us, event | category | flops | bytes accessed | tf_op | source)
XLA Modules:
  0.0 158.2 jit_solution(4470335550946866538)
XLA Ops:
  7.2 0.0 copy-start
  7.2 0.0 all-gather.3.cloned.1.call-start
  7.3 0.9 broadcast_compare_fusion
  8.1 1.8 %and_select_fusion.1 = bf16[2,256,256]{2,1,0:T(8,128)(2,1)} fusion(bf16[2,256,256]{2,1,0:T(8,128)(2,1)} %param.8, pred[2,256]{1,0:T(4,128)(4,1)S(1)} %get-tuple-element.20, pred[2,256]{1,0:T(4,128)(4,1)S(1)} %get-tuple-element.21), kind=kLoop, calls=%fused_computation.13 | loop fusion | flops 262144 | bytes 525312 | tf_op jit(solution)/shard_map/jit(_where)/select_n | solution.py:17
  9.9 0.0 all-gather.3.cloned.1.call-update
  10.0 0.0 all-gather.5.cloned.1.call-start
  10.0 1.5 fusion.31
  19.3 10.4 %all-gather.3.cloned.1.call-done = bf16[2,1024,256]{2,1,0:T(8,128)(2,1)} async-done(((bf16[2,256,256]{2,1,0:T(8,128)(2,1)}), bf16[2,1024,256]{2,1,0:T(8,128)(2,1)}) %all-gather.3.cloned.1.call-update) | async-done | bytes 1048592 | tf_op jit(solution)/shard_map/all_gather | solution.py:20
  29.6 0.0 copy-start.4
  29.6 0.0 copy-start.5
  29.6 1.7 %fusion = bf16[1,256,256]{1,2,0:T(8,128)(2,1)S(1)} fusion(bf16[4,256,1024]{2,1,0:T(8,128)(2,1)} %param.12, bf16[2,1024,256]{2,1,0:T(8,128)(2,1)} %all-gather.3.cloned.1.call-done, s32[]{:T(128)S(6)} %select_n.35), kind=kOutput, calls=%fused_computation.4 | convolution fusion | flops 134283264 | bytes 1179652 | tf_op jit(solution)/shard_map/dot_general | solution.py:25
  31.3 1.6 fusion.1
  32.9 0.0 copy-done.4
  32.9 0.0 copy-start.2
  32.9 1.4 fusion.2
  34.3 0.0 copy-done.5
  34.3 0.4 fusion.3
  34.7 0.9 pad_maximum_fusion
  35.6 0.0 all-gather.5.cloned.1.call-update
  35.6 0.0 all-reduce.3.cloned.1.call-start
  35.6 0.0 copy-done.2
  35.7 0.6 fusion.30
  36.2 1.1 iota_compare_fusion
  37.4 1.3 iota_compare_fusion.2
  38.7 42.7 %all-gather.5.cloned.1.call-done = bf16[4,256,1024]{1,2,0:T(8,128)(2,1)} async-done(((bf16[4,256,256]{1,2,0:T(8,128)(2,1)}), bf16[4,256,1024]{1,2,0:T(8,128)(2,1)}) %all-gather.5.cloned.1.call-update) | async-done | bytes 2097168 | tf_op jit(solution)/shard_map/all_gather | solution.py:32
  81.4 0.0 copy-done
  81.4 2.4 %fusion.32 = f32[4,256,256]{2,1,0:T(8,128)S(1)} fusion(bf16[4,256,1024]{1,2,0:T(8,128)(2,1)} %all-gather.5.cloned.1.call-done, bf16[4,256,1024]{2,1,0:T(8,128)(2,1)S(1)} %copy-done), kind=kOutput, calls=%fused_computation.56 | convolution fusion | flops 536870912 | bytes 5242880 | tf_op jit(solution)/shard_map/txl,tml->txm/dot_general | solution.py:30
  83.9 0.0 copy-start.1
  83.9 0.0 copy-start.3
  83.9 0.1 slice_bitcast_fusion.3
  84.0 1.0 select_add_fusion
  85.0 0.0 all-reduce.3.cloned.1.call-update
  85.0 27.6 %all-reduce.3.cloned.1.call-done = f32[2,256,256]{2,1,0:T(8,128)} async-done(((f32[2,256,256]{2,1,0:T(8,128)}), f32[2,256,256]{2,1,0:T(8,128)}) %all-reduce.3.cloned.1.call-update) | async-done | bytes 524304 | tf_op jit(solution)/shard_map/psum | solution.py:40
  112.6 0.0 copy-done.1
  112.6 0.0 copy-done.3
  112.6 2.0 %fusion.6 = (f32[]{:T(128)}, f32[]{:T(128)}) fusion(f32[2,256,256]{2,1,0:T(8,128)} %all-reduce.3.cloned.1.call-done, f32[2]{0:T(128)S(1)} %copy-done.3, pred[2,256]{1,0:T(4,128)(4,1)S(1)} %get-tuple-element.20, pred[2,256]{1,0:T(4,128)(4,1)S(1)} %get-tuple-element.21, bf16[2,256,256]{2,1,0:T(8,128)(2,1)S(1)} %copy-done.1), kind=kLoop, calls=%fused_computation.16 | loop fusion | flops 1310718 | bytes 787472 | tf_op jit(solution)/shard_map/reduce_sum | solution.py:43
  114.6 33.8 %all-reduce = (f32[]{:T(128)}, f32[]{:T(128)}) all-reduce(f32[]{:T(128)} %get-tuple-element.3, f32[]{:T(128)} %get-tuple-element.2), channel_id=1, replica_groups=mesh['terms'=2,'rows'=4,'cols'=4] {'rows','cols'}, use_global_device_ids=true, to_apply=%region_2.3 | all-reduce | flops 2 | bytes 16 | tf_op jit(solution)/shard_map/psum | solution.py:42
  149.6 2.1 %fusion.8 = (bf16[2,256,256]{2,1,0:T(8,128)(2,1)}, bf16[2,256,256]{2,1,0:T(8,128)(2,1)}) fusion(f32[]{:T(128)S(6)} %div.3, f32[2,256,256]{2,1,0:T(8,128)} %all-reduce.3.cloned.1.call-done, f32[2]{0:T(128)S(1)} %copy-done.3, pred[2,256]{1,0:T(4,128)(4,1)S(1)} %get-tuple-element.20, pred[2,256]{1,0:T(4,128)(4,1)S(1)} %get-tuple-element.21, ...), kind=kLoop, calls=%fused_computation.18 | loop fusion | flops 1310720 | bytes 1311756 | tf_op jit(solution)/shard_map/convert_element_type | solution.py:47
  (2 shorter events, 0.0 us)
Async XLA Ops:
  7.2 74.2 %copy-start = (bf16[4,256,1024]{2,1,0:T(8,128)(2,1)S(1)}, bf16[4,256,1024]{2,1,0:T(8,128)(2,1)}, u32[]{:S(2)}) copy-start(bf16[4,256,1024]{2,1,0:T(8,128)(2,1)} %param.13) | copy-start | bytes 6291460
  7.2 22.4 %all-gather.3.cloned.1.call-start = ((), (), s32[]{:S(2)}) async-start(), calls=%async_computation | async-start | bytes 1310720 | tf_op jit(solution)/shard_map/all_gather | solution.py:20
  10.0 71.4 %all-gather.5.cloned.1.call-start = ((), (), s32[]{:S(2)}) async-start(), calls=%async_computation.1 | async-start | bytes 2621440 | tf_op jit(solution)/shard_map/all_gather | solution.py:32
  29.6 3.3 %copy-start.4 = (bf16[4,256,1024]{2,1,0:T(8,128)(2,1)S(1)}, bf16[4,256,1024]{2,1,0:T(8,128)(2,1)}, u32[]{:S(2)}) copy-start(bf16[4,256,1024]{2,1,0:T(8,128)(2,1)} %param.12) | copy-start | bytes 6291460
  29.6 4.7 %copy-start.5 = (bf16[2,1024,256]{2,1,0:T(8,128)(2,1)S(1)}, bf16[2,1024,256]{2,1,0:T(8,128)(2,1)}, u32[]{:S(2)}) copy-start(bf16[2,1024,256]{2,1,0:T(8,128)(2,1)} %all-gather.3.cloned.1.call-done) | copy-start | bytes 3145732
  32.9 2.7 %copy-start.2 = (s32[4]{0:T(128)S(1)}, s32[4]{0:T(128)}, u32[]{:S(2)}) copy-start(s32[4]{0:T(128)} %param.15) | copy-start | bytes 52
  35.6 77.0 %all-reduce.3.cloned.1.call-start = ((), (), s32[]{:S(2)}) async-start(), calls=%async_computation.2 | async-start | bytes 1048576 | tf_op jit(solution)/shard_map/psum | solution.py:40
  83.9 28.7 %copy-start.1 = (bf16[2,256,256]{2,1,0:T(8,128)(2,1)S(1)}, bf16[2,256,256]{2,1,0:T(8,128)(2,1)}, u32[]{:S(2)}) copy-start(bf16[2,256,256]{2,1,0:T(8,128)(2,1)} %param.8) | copy-start | bytes 786436
  83.9 28.7 %copy-start.3 = (f32[2]{0:T(128)S(1)}, f32[2]{0:T(128)}, u32[]{:S(2)}) copy-start(f32[2]{0:T(128)} %param.9) | copy-start | bytes 28
Sparse Core Ops, SparseCore 0:
  10.1 19.4 all-gather.2
  35.7 45.6 all-gather.4
  85.1 27.4 all-reduce.2
where the time goes:
time: 159 us; the launch traced here: 158 us
  waiting for transfers between devices  80.8 us (51%)
  blocking collectives  33.8 us (21%)
  between operations  23 us (14%)
  other arithmetic  11 us (7%)
  matrix products  7.45 us (5%)
  local copies, waits for them, and re-layouts  2.17 us (1%)
    all_gather x1, waiting for transfers between devices, per_device(): lax.all_gather(products, 'cols', axis=2, tiled=True)  42.7 us
    psum x1, blocking collectives, per_device(): lax.psum((jnp.sum(live_f * full_sigma), jnp.sum(live_f * live_f)), ('rows...  33.8 us
    psum x1, waiting for transfers between devices, per_device(): summed = lax.psum(partial_value, 'terms')  27.6 us
    all_gather x1, waiting for transfers between devices, per_device(): panels = lax.all_gather(live_psi, 'rows', axis=1, tiled=True)  10.4 us
    dot_general x4, matrix products, per_device(): jnp.dot(left_ops[term_index], col_panel, preferred_element_type=jnp.float32)  5 us
  transfers between devices with their start and end apart: 3, of which 3 were waited for; matrix products, arithmetic and copies ran while one was open for 3% of the time, Pallas kernels for 0%

commit v1 on v0

--- a/solution.py
+++ b/solution.py
@@ -1,9 +1,18 @@
+import functools
 import jax
 import jax.numpy as jnp
 from jax import lax
 from jax.sharding import PartitionSpec as P
 
 EPSILON = 1e-06
+
+
+def choose_stops_all(chunk, across, a_name):
+    w1 = jax.lax.psum(jax.lax.psum(chunk, across), a_name)
+    return w1
+
+
+node_pack = functools.partial(choose_stops_all, across="cols", a_name="rows")
 
 
 def per_device(wavefunction, energy, block_rows, block_cols, left_ops, right_ops, source, target):
@@ -39,9 +48,7 @@
     live_f = live_psi.astype(jnp.float32)
     summed = lax.psum(partial_value, "terms")
     full_sigma = jnp.where(inside, summed + energy[:, None, None] * live_f, 0.0)
-    numerator, denominator = lax.psum(
-        (jnp.sum(live_f * full_sigma), jnp.sum(live_f * live_f)), ("rows", "cols")
-    )
+    numerator, denominator = node_pack((jnp.sum(live_f * full_sigma), jnp.sum(live_f * live_f)))
     rayleigh = numerator / (denominator + EPSILON)
     residual = full_sigma - rayleigh * live_f
     return (full_sigma.astype(jnp.bfloat16), residual.astype(jnp.bfloat16))

time: 159 us -> 144 us (0.906)
  blocking collectives: 33.8 us -> 18.6 us
    psum x1 -> x2, blocking collectives: 33.8 us -> 18.6 us  [choose_stops_all(): w1 = jax.lax.psum(jax.lax.psum(chunk, across), a_name)]
where the time goes in v1:
time: 144 us; the launch traced here: 143 us
  waiting for transfers between devices  80.8 us (56%)
  between operations  22.8 us (16%)
  blocking collectives  18.6 us (13%)
  other arithmetic  11.1 us (8%)
  matrix products  7.45 us (5%)
  local copies, waits for them, and re-layouts  2.2 us (2%)
    all_gather x1, waiting for transfers between devices, per_device(): lax.all_gather(products, 'cols', axis=2, tiled=True)  42.6 us
    psum x1, waiting for transfers between devices, per_device(): summed = lax.psum(partial_value, 'terms')  27.6 us
    psum x2, blocking collectives, choose_stops_all(): w1 = jax.lax.psum(jax.lax.psum(chunk, across), a_name)  18.6 us
    all_gather x1, waiting for transfers between devices, per_device(): panels = lax.all_gather(live_psi, 'rows', axis=1, tiled=True)  10.5 us
    dot_general x4, matrix products, per_device(): jnp.dot(left_ops[term_index], col_panel, preferred_element_type=jnp.float32)  5 us
  transfers between devices with their start and end apart: 3, of which 3 were waited for; matrix products, arithmetic and copies ran while one was open for 3% of the time, Pallas kernels for 0%

profile of v1, /device:TPU:0, one launch (start us, length us, event | category | flops | bytes accessed | tf_op | source)
XLA Modules:
  0.0 143.0 jit_solution(12156974984244579085)
XLA Ops:
  7.2 0.0 copy-start
  7.2 0.0 all-gather.3.cloned.1.call-start
  7.3 0.9 broadcast_compare_fusion
  8.1 1.8 %and_select_fusion.1 = bf16[2,256,256]{2,1,0:T(8,128)(2,1)} fusion(bf16[2,256,256]{2,1,0:T(8,128)(2,1)} %param.8, pred[2,256]{1,0:T(4,128)(4,1)S(1)} %get-tuple-element.22, pred[2,256]{1,0:T(4,128)(4,1)S(1)} %get-tuple-element.23), kind=kLoop, calls=%fused_computation.13 | loop fusion | flops 262144 | bytes 525312 | tf_op jit(solution)/shard_map/jit(_where)/select_n | solution.py:26
  9.9 0.0 all-gather.3.cloned.1.call-update
  10.0 0.0 all-gather.5.cloned.1.call-start
  10.0 1.5 %fusion.31 = (s32[1]{0:T(128)}, s32[1]{0:T(128)}, s32[1]{0:T(128)}, s32[1]{0:T(128)}) fusion(s32[4]{0:T(128)} %param.14), kind=kLoop, calls=%fused_computation.55 | loop fusion | bytes 32 | tf_op jit(solution)/shard_map/slice | solution.py:32
  19.1 10.5 %all-gather.3.cloned.1.call-done = bf16[2,1024,256]{2,1,0:T(8,128)(2,1)} async-done(((bf16[2,256,256]{2,1,0:T(8,128)(2,1)}), bf16[2,1024,256]{2,1,0:T(8,128)(2,1)}) %all-gather.3.cloned.1.call-update) | async-done | bytes 1048592 | tf_op jit(solution)/shard_map/all_gather | solution.py:29
  29.6 0.0 copy-start.4
  29.6 0.0 copy-start.5
  29.6 1.7 %fusion = bf16[1,256,256]{1,2,0:T(8,128)(2,1)S(1)} fusion(bf16[4,256,1024]{2,1,0:T(8,128)(2,1)} %param.12, bf16[2,1024,256]{2,1,0:T(8,128)(2,1)} %all-gather.3.cloned.1.call-done, s32[]{:T(128)S(6)} %select_n.35), kind=kOutput, calls=%fused_computation.4 | convolution fusion | flops 134283264 | bytes 1179652 | tf_op jit(solution)/shard_map/dot_general | solution.py:34
  31.3 1.6 %fusion.1 = bf16[1,256,256]{1,2,0:T(8,128)(2,1)S(1)} fusion(bf16[4,256,1024]{2,1,0:T(8,128)(2,1)} %param.12, bf16[2,1024,256]{2,1,0:T(8,128)(2,1)} %all-gather.3.cloned.1.call-done, s32[]{:T(128)S(6)} %select_n.36), kind=kOutput, calls=%fused_computation.5 | convolution fusion | flops 134283264 | bytes 1179652 | tf_op jit(solution)/shard_map/dot_general | solution.py:34
  32.9 0.0 copy-done.4
  32.9 0.0 copy-start.2
  32.9 1.4 fusion.2
  34.3 0.0 copy-done.5
  34.3 0.4 fusion.3
  34.7 0.9 pad_maximum_fusion
  35.6 0.0 all-gather.5.cloned.1.call-update
  35.6 0.0 all-reduce.4.cloned.1.call-start
  35.6 0.0 copy-done.2
  35.6 0.6 fusion.30
  36.3 1.2 iota_compare_fusion
  37.5 1.3 iota_compare_fusion.2
  38.8 42.6 %all-gather.5.cloned.1.call-done = bf16[4,256,1024]{1,2,0:T(8,128)(2,1)} async-done(((bf16[4,256,256]{1,2,0:T(8,128)(2,1)}), bf16[4,256,1024]{1,2,0:T(8,128)(2,1)}) %all-gather.5.cloned.1.call-update) | async-done | bytes 2097168 | tf_op jit(solution)/shard_map/all_gather | solution.py:41
  81.4 0.0 copy-done
  81.4 2.4 %fusion.32 = f32[4,256,256]{2,1,0:T(8,128)S(1)} fusion(bf16[4,256,1024]{1,2,0:T(8,128)(2,1)} %all-gather.5.cloned.1.call-done, bf16[4,256,1024]{2,1,0:T(8,128)(2,1)S(1)} %copy-done), kind=kOutput, calls=%fused_computation.56 | convolution fusion | flops 536870912 | bytes 5242880 | tf_op jit(solution)/shard_map/txl,tml->txm/dot_general | solution.py:39
  83.9 0.0 copy-start.1
  83.9 0.0 copy-start.3
  83.9 0.1 slice_bitcast_fusion.3
  84.0 1.0 select_add_fusion
  84.9 0.0 all-reduce.4.cloned.1.call-update
  85.0 27.6 %all-reduce.4.cloned.1.call-done = f32[2,256,256]{2,1,0:T(8,128)} async-done(((f32[2,256,256]{2,1,0:T(8,128)}), f32[2,256,256]{2,1,0:T(8,128)}) %all-reduce.4.cloned.1.call-update) | async-done | bytes 524304 | tf_op jit(solution)/shard_map/psum | solution.py:49
  112.6 0.0 copy-done.1
  112.6 0.0 copy-done.3
  112.6 2.0 %fusion.6 = (f32[]{:T(128)}, f32[]{:T(128)}) fusion(f32[2,256,256]{2,1,0:T(8,128)} %all-reduce.4.cloned.1.call-done, f32[2]{0:T(128)S(1)} %copy-done.3, pred[2,256]{1,0:T(4,128)(4,1)S(1)} %get-tuple-element.22, pred[2,256]{1,0:T(4,128)(4,1)S(1)} %get-tuple-element.23, bf16[2,256,256]{2,1,0:T(8,128)(2,1)S(1)} %copy-done.1), kind=kLoop, calls=%fused_computation.16 | loop fusion | flops 1310718 | bytes 787472 | tf_op jit(solution)/shard_map/reduce_sum | solution.py:51
  114.5 12.3 %all-reduce = (f32[]{:T(128)}, f32[]{:T(128)}) all-reduce(f32[]{:T(128)} %get-tuple-element.3, f32[]{:T(128)} %get-tuple-element.2), channel_id=1, replica_groups=mesh['terms'=2,'rows'=4,'cols'=4] {'cols'}, use_global_device_ids=true, to_apply=%region_2.3 | all-reduce | flops 2 | bytes 16 | tf_op jit(solution)/shard_map/psum | solution.py:11
  126.8 6.3 %all-reduce.1 = (f32[]{:T(128)}, f32[]{:T(128)}) all-reduce(f32[]{:T(128)} %get-tuple-element.4, f32[]{:T(128)} %get-tuple-element.5), channel_id=1, replica_groups=mesh['terms'=2,'rows'=4,'cols'=4] {'rows'}, use_global_device_ids=true, to_apply=%region_3.4 | all-reduce | flops 2 | bytes 16 | tf_op jit(solution)/shard_map/psum | solution.py:11
  134.4 2.1 %fusion.8 = (bf16[2,256,256]{2,1,0:T(8,128)(2,1)}, bf16[2,256,256]{2,1,0:T(8,128)(2,1)}) fusion(f32[]{:T(128)S(6)} %div.3, f32[2,256,256]{2,1,0:T(8,128)} %all-reduce.4.cloned.1.call-done, f32[2]{0:T(128)S(1)} %copy-done.3, pred[2,256]{1,0:T(4,128)(4,1)S(1)} %get-tuple-element.22, pred[2,256]{1,0:T(4,128)(4,1)S(1)} %get-tuple-element.23, ...), kind=kLoop, calls=%fused_computation.18 | loop fusion | flops 1310720 | bytes 1311756 | tf_op jit(solution)/shard_map/convert_element_type | solution.py:54
  (2 shorter events, 0.0 us)
Async XLA Ops:
  7.2 74.2 %copy-start = (bf16[4,256,1024]{2,1,0:T(8,128)(2,1)S(1)}, bf16[4,256,1024]{2,1,0:T(8,128)(2,1)}, u32[]{:S(2)}) copy-start(bf16[4,256,1024]{2,1,0:T(8,128)(2,1)} %param.13) | copy-start | bytes 6291460
  7.2 22.4 %all-gather.3.cloned.1.call-start = ((), (), s32[]{:S(2)}) async-start(), calls=%async_computation | async-start | bytes 1310720 | tf_op jit(solution)/shard_map/all_gather | solution.py:29
  10.0 71.4 %all-gather.5.cloned.1.call-start = ((), (), s32[]{:S(2)}) async-start(), calls=%async_computation.1 | async-start | bytes 2621440 | tf_op jit(solution)/shard_map/all_gather | solution.py:41
  29.6 3.3 %copy-start.4 = (bf16[4,256,1024]{2,1,0:T(8,128)(2,1)S(1)}, bf16[4,256,1024]{2,1,0:T(8,128)(2,1)}, u32[]{:S(2)}) copy-start(bf16[4,256,1024]{2,1,0:T(8,128)(2,1)} %param.12) | copy-start | bytes 6291460
  29.6 4.7 %copy-start.5 = (bf16[2,1024,256]{2,1,0:T(8,128)(2,1)S(1)}, bf16[2,1024,256]{2,1,0:T(8,128)(2,1)}, u32[]{:S(2)}) copy-start(bf16[2,1024,256]{2,1,0:T(8,128)(2,1)} %all-gather.3.cloned.1.call-done) | copy-start | bytes 3145732
  32.9 2.7 %copy-start.2 = (s32[4]{0:T(128)S(1)}, s32[4]{0:T(128)}, u32[]{:S(2)}) copy-start(s32[4]{0:T(128)} %param.15) | copy-start | bytes 52
  35.6 77.0 %all-reduce.4.cloned.1.call-start = ((), (), s32[]{:S(2)}) async-start(), calls=%async_computation.2 | async-start | bytes 1048576 | tf_op jit(solution)/shard_map/psum | solution.py:49
  83.9 28.7 %copy-start.1 = (bf16[2,256,256]{2,1,0:T(8,128)(2,1)S(1)}, bf16[2,256,256]{2,1,0:T(8,128)(2,1)}, u32[]{:S(2)}) copy-start(bf16[2,256,256]{2,1,0:T(8,128)(2,1)} %param.8) | copy-start | bytes 786436
  83.9 28.7 %copy-start.3 = (f32[2]{0:T(128)S(1)}, f32[2]{0:T(128)}, u32[]{:S(2)}) copy-start(f32[2]{0:T(128)} %param.9) | copy-start | bytes 28
Sparse Core Ops, SparseCore 0:
  10.1 19.4 all-gather.2
  35.7 45.6 all-gather.4
  85.1 27.4 all-reduce.3
